TPU v7x, 32 devices: a 4x2x2 block of a 4x4x8 slice. The times are simulated.
32 devices in a mesh: dp: 4 (over y, z), sp: 8 (over x, core).
Axes of the slice: x: 4, y: 2, z: 2, core: 2. Of those that a mesh axis runs over, the one named last changes fastest.
The devices are a block of a 4x4x8 slice.
Arguments:
- hidden: bfloat16 [8192, 4096], P(('dp', 'sp')), parts along dimension 0
- w_q: bfloat16 [4096, 4096], replicated
- w_k: bfloat16 [4096, 1024], replicated
- w_v: bfloat16 [4096, 1024], replicated
- w_o: bfloat16 [4096, 4096], replicated
- expert_ids: int32 [8192, 2], P(('dp', 'sp')), parts along dimension 0
- router_probs: float32 [8192, 16], P(('dp', 'sp')), parts along dimension 0
Outputs:
- output 1: bfloat16 [8192, 4096], P(('dp', 'sp')), parts along dimension 0
- output 2: bfloat16 [64, 2048, 4096], P(('dp', 'sp')), parts along dimension 0
There are 4 independent parts. A program takes and returns all parts, laid end to end along the dimension named above; an argument that names none is the same for every part.
All inputs are finite; a program needn't handle non-finite values.
Results may differ from a plain program's by a relative error of at most 0.00968718.
Values are sent between devices in bfloat16 or wider.
A program may use at most 768 MiB of HBM per device.

v0:
```python
import math
import jax
import jax.numpy as jnp
from jax import lax
from jax.sharding import PartitionSpec as P

HEAD_DIM = 128
SCORE_SCALE = 1.0 / math.sqrt(HEAD_DIM)


def route_rows(hidden_out, expert_ids, router_probs):
    tok_dev, width = hidden_out.shape
    experts = router_probs.shape[1]
    picked = jnp.take_along_axis(router_probs, expert_ids, axis=1)
    gate_w = picked / jnp.sum(picked, axis=1, keepdims=True)
    gated = (gate_w[:, :, None] * hidden_out[:, None, :].astype(jnp.float32)).astype(jnp.bfloat16)
    token_hits = jnp.sum((expert_ids[:, :, None] == jnp.arange(experts)).astype(jnp.int32), axis=1)
    earlier = jnp.cumsum(token_hits, axis=0) - token_hits
    slot_rank = jnp.take_along_axis(earlier, expert_ids, axis=1)
    send_buf = jnp.zeros((experts, tok_dev, width), jnp.bfloat16)
    return send_buf.at[expert_ids, slot_rank].set(gated, unique_indices=True)


def solution(mesh):
    group = mesh.shape['sp']
    row_spec = P(('dp', 'sp'), None)
    buf_spec = P(('dp', 'sp'), None, None)

    def device_step(x_loc, w_q, w_k, w_v, w_o, ids_loc, probs_loc):
        tok_dev = x_loc.shape[0]
        seq_len = tok_dev * group
        n_heads = w_q.shape[1] // HEAD_DIM
        kv_heads = w_k.shape[1] // HEAD_DIM
        kv_copies = max(1, group // kv_heads)
        head_dev = n_heads // group
        kv_dev = kv_heads * kv_copies // group
        q_loc = jnp.dot(x_loc, w_q, preferred_element_type=jnp.float32).astype(jnp.bfloat16).reshape(tok_dev, n_heads, HEAD_DIM)
        k_loc = jnp.dot(x_loc, w_k, preferred_element_type=jnp.float32).astype(jnp.bfloat16).reshape(tok_dev, kv_heads, HEAD_DIM)
        v_loc = jnp.dot(x_loc, w_v, preferred_element_type=jnp.float32).astype(jnp.bfloat16).reshape(tok_dev, kv_heads, HEAD_DIM)
        k_loc = jnp.repeat(k_loc, kv_copies, axis=1)
        v_loc = jnp.repeat(v_loc, kv_copies, axis=1)
        q_seq = lax.all_to_all(q_loc, 'sp', 1, 0, tiled=True)
        k_seq = lax.all_to_all(k_loc, 'sp', 1, 0, tiled=True)
        v_seq = lax.all_to_all(v_loc, 'sp', 1, 0, tiled=True)
        q_grp = q_seq.reshape(seq_len, kv_dev, head_dev // kv_dev, HEAD_DIM)
        scores = jnp.einsum('qgmd,kgd->gmqk', q_grp, k_seq, preferred_element_type=jnp.float32) * SCORE_SCALE
        positions = jnp.arange(seq_len)
        causal = positions[:, None] >= positions[None, :]
        weights = jax.nn.softmax(jnp.where(causal, scores, -1e30), axis=-1).astype(jnp.bfloat16)
        attn_seq = jnp.einsum('gmqk,kgd->qgmd', weights, v_seq, preferred_element_type=jnp.float32).astype(jnp.bfloat16)
        attn_seq = attn_seq.reshape(seq_len, head_dev, HEAD_DIM)
        attn_loc = lax.all_to_all(attn_seq, 'sp', 0, 1, tiled=True).reshape(tok_dev, n_heads * HEAD_DIM)
        out_proj = jnp.dot(attn_loc, w_o, preferred_element_type=jnp.float32)
        hidden_out = (x_loc.astype(jnp.float32) + out_proj).astype(jnp.bfloat16)
        send_buf = route_rows(hidden_out, ids_loc, probs_loc)
        recv_buf = lax.all_to_all(send_buf, 'sp', 0, 1, tiled=True)
        return hidden_out, recv_buf

    return jax.shard_map(device_step, mesh=mesh, in_specs=(row_spec, P(), P(), P(), P(), row_spec, row_spec), out_specs=(row_spec, buf_spec), check_vma=False)
```

profile of v0, /device:TPU:81, one launch (start us, length us, event | category | flops | bytes accessed | tf_op | source)
XLA Modules:
  0.0 759.9 jit_solution(5950055387760497359)
XLA Ops:
  0.6 15.7 %fusion.11 = bf16[32,32,8,128]{3,2,1,0:T(8,128)(2,1)S(1)} fusion(bf16[256,4096]{1,0:T(8,128)(2,1)} %param.7, bf16[4096,4096]{1,0:T(8,128)(2,1)} %param.8), kind=kOutput, calls=%fused_computation.18 | convolution fusion | flops 8590983168 | bytes 37748736 | tf_op jit(solution)/shard_map/dot_general | solution.py:37
  16.3 1.9 copy.134
  18.2 6.0 all-to-all-start.2
  24.2 6.5 fusion.13
  30.7 0.9 copy.135
  31.6 5.8 fusion.12
  37.4 0.9 copy.136
  38.3 11.9 %all-to-all-done.2 = bf16[256,32,128]{2,0,1:T(8,128)(2,1)S(1)} async-done(((bf16[256,32,128]{2,0,1:T(8,128)(2,1)}), bf16[256,32,128]{2,0,1:T(8,128)(2,1)S(1)}, u32[]{:S(2)}, u32[]{:S(2)}) %all-to-all-start.2) | async-done | bytes 2097184 | tf_op jit(solution)/shard_map/all_to_all | solution.py:42
  50.2 4.6 all-to-all-start.1
  54.8 4.1 iota_compare_fusion
  59.0 1.5 copy.107
  60.4 3.6 all-to-all-done.1
  64.1 4.6 all-to-all-start
  68.7 26.5 %fusion.1 = (f32[4,2048]{1,0:T(4,128)S(1)}, f32[2048,2048,4]{1,0,2:T(8,128)}) fusion(pred[2048,2048]{0,1:T(8,128)(4,1)} %iota_compare_fusion, bf16[2048,128,1]{1,0,2:T(8,128)(2,1)S(1)} %bitcast.111, bf16[2048,4,128]{2,0,1:T(8,128)(2,1)} %bitcast.110), kind=kOutput, calls=%fused_computation.7 | convolution fusion | flops 4345290752 | bytes 73957376 | tf_op jit(solution)/shard_map/qgmd,kgd->gmqk/dot_general | solution.py:46
  95.2 22.9 %fusion = f32[4,2048]{1,0:T(4,128)S(1)} fusion(f32[2048,2048,4]{1,0,2:T(8,128)} %get-tuple-element.3, f32[4,2048]{1,0:T(4,128)S(1)} %get-tuple-element.2, pred[2048,2048]{0,1:T(8,128)(4,1)} %iota_compare_fusion), kind=kLoop, calls=%fused_computation.6 | loop fusion | flops 67100672 | bytes 71368704 | tf_op jit(solution)/shard_map/reduce_sum | solution.py:49
  118.1 28.1 %fusion.8 = bf16[2048,4,128]{0,2,1:T(8,128)(2,1)S(1)} fusion(bf16[2048,128,1]{1,0,2:T(8,128)(2,1)S(1)} %bitcast.112, f32[4,2048]{1,0:T(4,128)S(1)} %fusion, f32[4,2048]{1,0:T(4,128)S(1)} %get-tuple-element.2, f32[2048,2048,4]{1,0,2:T(8,128)} %get-tuple-element.3, pred[2048,2048]{0,1:T(8,128)(4,1)} %iota_compare_fusion), kind=kOutput, calls=%fused_computation.16 | convolution fusion | flops 4379901952 | bytes 73990144 | tf_op jit(solution)/shard_map/gmqk,kgd->qgmd/dot_general | solution.py:50
  146.2 2.5 copy.109
  148.8 4.9 all-to-all-start.3
  154.0 4.5 gather_fusion.1
  159.1 0.6 reduce-window.6
  159.6 0.2 slice_reduce_fusion
  160.1 3.8 gather_fusion
  164.4 15.2 %all-to-all-done.3 = bf16[2048,4,128]{2,1,0:T(4,128)(2,1)S(1)} async-done(((bf16[2048,4,128]{2,1,0:T(4,128)(2,1)}), bf16[2048,4,128]{2,1,0:T(4,128)(2,1)S(1)}, u32[]{:S(2)}, u32[]{:S(2)}) %all-to-all-start.3) | async-done | bytes 2097184 | tf_op jit(solution)/shard_map/all_to_all | solution.py:52
  179.6 1.6 copy.110
  181.2 2.9 copy.111
  184.1 16.6 %fusion.20 = (f32[256,4096]{1,0:T(8,128)S(1)}, bf16[256,4096]{1,0:T(8,128)(2,1)}) fusion(bf16[256,4096]{0,1:T(8,128)(2,1)S(1)} %bitcast.106, bf16[4096,4096]{1,0:T(8,128)(2,1)} %param.11, bf16[256,4096]{1,0:T(8,128)(2,1)} %param.7), kind=kOutput, calls=%fused_computation.46 | convolution fusion | flops 8594128896 | bytes 44040192 | tf_op jit(solution)/shard_map/dot_general | solution.py:53
  200.7 5.5 multiply_convert_fusion
  206.1 7.2 reshape.107
  213.3 11.1 %broadcast_in_dim.34 = bf16[16,256,4096]{2,1,0:T(8,128)(2,1)} broadcast(bf16[]{:T(256)} %constant.25.clone.1), dimensions={} | broadcast | bytes 33554432 | tf_op jit(solution)/shard_map/broadcast_in_dim | solution.py:20
  224.5 136.9 %scatter_fusion = bf16[16,256,4096]{2,1,0:T(8,128)(2,1)} fusion(bf16[16,256,4096]{2,1,0:T(8,128)(2,1)} %broadcast_in_dim.34, s32[512]{0:T(512)S(1)} %reshape.105, bf16[512,4096]{1,0:T(8,128)(2,1)} %reshape.107), kind=kCustom, calls=%fused_computation.2 | custom fusion | bytes 12587008 | tf_op jit(solution)/shard_map/scatter | solution.py:21
  361.4 375.4 %all_to_all.78 = bf16[16,256,4096]{2,1,0:T(8,128)(2,1)} all-to-all(bf16[16,256,4096]{2,1,0:T(8,128)(2,1)} %scatter_fusion), channel_id=1, replica_groups=mesh['dp'=4,'sp'=8] {'sp'}, dimensions={0} | all-to-all | bytes 67108864 | tf_op jit(solution)/shard_map/all_to_all | solution.py:56
  736.8 22.9 %copy.121 = bf16[2,8,256,4096]{3,2,1,0:T(8,128)(2,1)} copy(bf16[2,8,256,4096]{3,2,0,1:T(8,128)(2,1)} %bitcast.104) | data formatting | bytes 67108864 | tf_op jit(solution)/shard_map/all_to_all | solution.py:56
  (30 shorter events, 1.6 us)
Async XLA Ops:
  0.6 153.3 %copy-start = (f32[256,16]{0,1:T(8,128)S(1)}, f32[256,16]{0,1:T(8,128)}, u32[]{:S(2)}) copy-start(f32[256,16]{0,1:T(8,128)} %param.13) | copy-start | bytes 49156
  18.2 32.0 %all-to-all-start.2 = ((bf16[256,32,128]{2,0,1:T(8,128)(2,1)}), bf16[256,32,128]{2,0,1:T(8,128)(2,1)S(1)}, u32[]{:S(2)}, u32[]{:S(2)}) async-start(bf16[256,32,128]{2,0,1:T(8,128)(2,1)} %bitcast.108), calls=%async_computation.2 | async-start | bytes 4194304 | tf_op jit(solution)/shard_map/all_to_all | solution.py:42
  24.2 7.4 copy-start.2
  50.2 13.8 %all-to-all-start.1 = ((bf16[256,8,128]{2,0,1:T(8,128)(2,1)}), bf16[256,8,128]{2,0,1:T(8,128)(2,1)S(1)}, u32[]{:S(2)}, u32[]{:S(2)}) async-start(bf16[256,8,128]{2,0,1:T(8,128)(2,1)} %bitcast.102), calls=%async_computation.1 | async-start | bytes 1048576 | tf_op jit(solution)/shard_map/all_to_all | solution.py:43
  64.1 54.0 %all-to-all-start = ((bf16[256,8,128]{2,0,1:T(8,128)(2,1)}), bf16[256,8,128]{2,0,1:T(8,128)(2,1)S(1)}, u32[]{:S(2)}, u32[]{:S(2)}) async-start(bf16[256,8,128]{2,0,1:T(8,128)(2,1)} %bitcast.103), calls=%async_computation | async-start | bytes 1048576 | tf_op jit(solution)/shard_map/all_to_all | solution.py:44
  146.2 7.4 copy-start.3
  148.8 30.9 %all-to-all-start.3 = ((bf16[2048,4,128]{2,1,0:T(4,128)(2,1)}), bf16[2048,4,128]{2,1,0:T(4,128)(2,1)S(1)}, u32[]{:S(2)}, u32[]{:S(2)}) async-start(bf16[2048,4,128]{2,1,0:T(4,128)(2,1)} %copy.109), calls=%async_computation.3 | async-start | bytes 4194304 | tf_op jit(solution)/shard_map/all_to_all | solution.py:52
  736.8 22.9 %copy-start.1 = (f32[256,16]{0,1:T(8,128)S(1)}, f32[256,16]{0,1:T(8,128)}, u32[]{:S(2)}) copy-start(f32[256,16]{0,1:T(8,128)} %param.13) | copy-start | bytes 49156
where the time goes:
time: 762 us; the launch traced here: 760 us
  blocking collectives  375 us (49%)
  local copies, waits for them, and re-layouts  200 us (26%)
  matrix products  99.1 us (13%)
  other arithmetic  33.3 us (4%)
  waiting for transfers between devices  30.8 us (4%)
  starting transfers between devices  20.1 us (3%)
    all_to_all x1, blocking collectives, device_step(): recv_buf = lax.all_to_all(send_buf, 'sp', 0, 1, tiled=True)  375 us
    scatter x1, local copies, waits for them, and re-layouts, route_rows(): return send_buf.at[expert_ids, slot_rank].set(gated, unique_indices=True)  137 us
    dot_general x1, matrix products, device_step(): jnp.einsum('gmqk,kgd->qgmd', weights, v_seq, preferred_element_type=jnp.f...  28.1 us
    dot_general x1, matrix products, device_step(): jnp.einsum('qgmd,kgd->gmqk', q_grp, k_seq, preferred_element_type=jnp.flo...  26.5 us
    reduce_sum x1, other arithmetic, device_step(): jax.nn.softmax(jnp.where(causal, scores, -1e+30), axis=-1)  22.9 us
    all_to_all x1, local copies, waits for them, and re-layouts, device_step(): recv_buf = lax.all_to_all(send_buf, 'sp', 0, 1, tiled=True)  22.9 us
    dot_general x1, matrix products, device_step(): out_proj = jnp.dot(attn_loc, w_o, preferred_element_type=jnp.float32)  16.6 us
    dot_general x1, matrix products, device_step(): jnp.dot(x_loc, w_q, preferred_element_type=jnp.float32).astype(jnp.bfloat16)  15.7 us
  transfers between devices with their start and end apart: 4, of which 3 were waited for; matrix products, arithmetic and copies ran while one was open for 10% of the time, Pallas kernels for 0%

commit v1 on v0

v1 whole, which is shorter than its diff:
```python
import functools
import math

import jax
import jax.numpy as jnp
from jax import lax
from jax.experimental import pallas as pl
from jax.experimental.pallas import tpu as pltpu
from jax.sharding import PartitionSpec as P

HEAD = 128
EXP2_SCALE = math.log2(math.e) / math.sqrt(HEAD)
MESH = pl.DeviceIdType.MESH
TILE = 512
SLOTS = 8
PER_TILE = TILE // HEAD
VMEM_LIMIT = 67_000_000


def block_kernel(group, n_exp, x_hbm, wq, wk, wv, wo, ids_ref, probs_ref, h_all, meta_all,
                 xb, wbuf, kv, q_s, acc, ml, o_s, h_s, meta_s,
                 x_sem, w_sem, k_send, kr_l, kr_r, kr_o, kr_p, h_send, hr_l, hr_r, hr_o, hr_p, m_send, m_recv, m_loc):
    tok = xb.shape[0]
    q_tiles = wq.shape[1] // TILE
    kv_tiles = 2 * wk.shape[1] // TILE
    k_tiles = kv_tiles // 2
    o_tiles = wo.shape[1] // TILE
    me = lax.axis_index("sp")
    core = lax.rem(me, 2)
    chip = lax.div(me, 2)
    right = lax.rem(me + 2, group)
    left = lax.rem(me + group - 2, group)
    partner = me + 1 - 2 * core
    opp = lax.rem(me + 4, group)
    own = pl.ds(0, tok)
    other = pl.ds(tok, tok)

    def remote(src, dst, send, recv, dev):
        return pltpu.make_async_remote_copy(src_ref=src, dst_ref=dst, send_sem=send, recv_sem=recv,
                                            device_id={"sp": dev}, device_id_type=MESH)

    def got(ref, sem):
        pltpu.make_async_copy(ref, ref, sem).wait()

    def w_copy(arr, col, slot):
        if not isinstance(col, int):
            col = pl.multiple_of(col, TILE)
        return pltpu.make_async_copy(arr.at[:, pl.ds(col, TILE)], wbuf.at[slot], w_sem.at[slot])

    x_copy = pltpu.make_async_copy(x_hbm, xb, x_sem)
    x_copy.start()
    for p in range(SLOTS):
        if p < k_tiles:
            w_copy(wk, p * TILE, p).start()
        elif p < kv_tiles:
            w_copy(wv, (p - k_tiles) * TILE, p).start()
        else:
            w_copy(wq, (p - kv_tiles) * TILE, p).start()

    barrier = pltpu.get_barrier_semaphore()
    for d in range(1, group):
        pl.semaphore_signal(barrier, inc=1, device_id={"sp": lax.rem(me + d, group)}, device_id_type=MESH)
    x_copy.wait()

    def kv_tile(p, carry):
        w_copy(wk, 0, p).wait()
        y = jnp.dot(xb[...], wbuf[p], preferred_element_type=jnp.float32).astype(jnp.bfloat16)
        for h in range(PER_TILE):
            kv[0, p, h, 0:tok, :] = y[:, h * HEAD:(h + 1) * HEAD]
        w_copy(wq, (SLOTS - kv_tiles + p) * TILE, p).start()

        @pl.when(p == 0)
        def _():
            pl.semaphore_wait(barrier, group - 1)

        src = kv.at[0, p, :, own, :]
        remote(src, kv.at[3, p, :, own, :], k_send.at[0], kr_l.at[p], right).start()
        remote(src, kv.at[1, p, :, own, :], k_send.at[1], kr_r.at[p], left).start()
        remote(src, kv.at[0, p, :, other, :], k_send.at[2], kr_p.at[0], partner).start()
        return carry

    lax.fori_loop(0, kv_tiles, kv_tile, 0)

    def q_tile(n, carry):
        slot = lax.rem(kv_tiles + n, SLOTS)
        w_copy(wq, 0, slot).wait()
        y = jnp.dot(xb[...], wbuf[slot], preferred_element_type=jnp.float32).astype(jnp.bfloat16)
        for h in range(PER_TILE):
            q_s[n, h * tok:(h + 1) * tok, :] = y[:, h * HEAD:(h + 1) * HEAD]
        w_copy(wo, n * TILE, slot).start()
        return carry

    lax.fori_loop(0, q_tiles, q_tile, 0)

    def to_partner_kv(r, p):
        remote(kv.at[r, p, :, own, :], kv.at[r, p, :, other, :], k_send.at[2 + r], kr_p.at[r], partner).start()

    for p in range(k_tiles):
        got(kv.at[3, p, :, own, :], kr_l.at[p])
        remote(kv.at[3, p, :, own, :], kv.at[2, p, :, own, :], k_send.at[6], kr_o.at[p], right).start()
        to_partner_kv(3, p)

    lane_e = lax.broadcasted_iota(jnp.int32, (tok, n_exp), 1)
    lane = lax.broadcasted_iota(jnp.int32, (tok, HEAD), 1)
    id0 = ids_ref[:, 0:1]
    id1 = ids_ref[:, 1:2]
    probs = probs_ref[...]
    p0 = jnp.sum(jnp.where(lane_e == id0, probs, 0.0), axis=1, keepdims=True)
    p1 = jnp.sum(jnp.where(lane_e == id1, probs, 0.0), axis=1, keepdims=True)
    total = p0 + p1
    hits = (lane == id0) | (lane == id1)
    before = (lax.broadcasted_iota(jnp.int32, (tok, tok), 1)
              < lax.broadcasted_iota(jnp.int32, (tok, tok), 0)).astype(jnp.float32).astype(jnp.bfloat16)
    earlier = jnp.dot(before, hits.astype(jnp.float32).astype(jnp.bfloat16), preferred_element_type=jnp.float32)
    slot_of = jnp.where(hits, earlier, -1.0)
    gate_of = jnp.where(lane == id0 + n_exp, p0 / total, jnp.where(lane == id1 + n_exp, p1 / total, 0.0))
    meta = jnp.transpose(jnp.where(lane < n_exp, slot_of, gate_of))
    meta_s[...] = meta[0:2 * n_exp, :]

    row_i = lax.broadcasted_iota(jnp.int32, (tok, tok), 0)
    col_i = lax.broadcasted_iota(jnp.int32, (tok, tok), 1)

    def attend(r, keys, first=False, diagonal=False):
        def head_group(g, carry):
            kp = lax.div(g, PER_TILE)
            kh = lax.rem(g, PER_TILE)
            k = kv[r, kp, kh, keys, :]
            v = kv[r, k_tiles + kp, kh, keys, :]
            for h in range(PER_TILE):
                rows = pl.ds(h * tok, tok)
                s = lax.dot_general(q_s[g, rows, :], k, (((1,), (1,)), ((), ())), preferred_element_type=jnp.float32)
                if diagonal:
                    s = jnp.where(row_i >= col_i, s, -1e30)
                top = jnp.max(s, axis=1, keepdims=True)
                if not first:
                    old = ml[g, rows, 0:1]
                    top = jnp.maximum(old, top)
                e = jnp.exp2((s - top) * EXP2_SCALE)
                mass = jnp.sum(e, axis=1, keepdims=True)
                out = jnp.dot(e.astype(jnp.bfloat16), v, preferred_element_type=jnp.float32)
                if not first:
                    keep = jnp.exp2((old - top) * EXP2_SCALE)
                    mass = mass + keep * ml[g, rows, 1:2]
                    out = out + keep * acc[g, rows, :]
                ml[g, rows, 0:1] = top
                ml[g, rows, 1:2] = mass
                acc[g, rows, :] = out
            return carry

        lax.fori_loop(0, q_tiles, head_group, 0)

    attend(0, own, first=True, diagonal=True)

    m_rows = meta_all.at[me]
    loc = pltpu.make_async_copy(meta_s, m_rows, m_loc)
    loc.start()
    for d in range(1, group):
        remote(meta_s, m_rows, m_send.at[d - 1], m_recv.at[d - 1], lax.rem(me + d, group)).start()

    got(kv.at[0, :, :, other, :], kr_p.at[0])

    @pl.when(core == 1)
    def _():
        attend(0, other)

    for p in range(kv_tiles):
        got(kv.at[1, p, :, own, :], kr_r.at[p])
        if p >= k_tiles:
            remote(kv.at[1, p, :, own, :], kv.at[2, p, :, own, :], k_send.at[7], kr_o.at[p], left).start()
            got(kv.at[3, p, :, own, :], kr_l.at[p])
            to_partner_kv(3, p)
        to_partner_kv(1, p)

    both = pl.ds(0, 2 * tok)
    got(kv.at[3, :, :, other, :], kr_p.at[3])

    @pl.when(chip >= 1)
    def _():
        attend(3, both)

    got(kv.at[1, :, :, other, :], kr_p.at[1])

    @pl.when(right < me)
    def _():
        attend(1, both)

    for p in range(kv_tiles):
        got(kv.at[2, p, :, own, :], kr_o.at[p])
        to_partner_kv(2, p)
    got(kv.at[2, :, :, other, :], kr_p.at[2])

    @pl.when(chip >= 2)
    def _():
        attend(2, both)

    def finish(g, carry):
        for h in range(PER_TILE):
            rows = pl.ds(h * tok, tok)
            o_s[:, pl.ds(pl.multiple_of(g * TILE + h * HEAD, HEAD), HEAD)] = (
                acc[g, rows, :] / ml[g, rows, 1:2]).astype(jnp.bfloat16)
        return carry

    lax.fori_loop(0, q_tiles, finish, 0)

    def rows_of(dev):
        return pl.ds(pl.multiple_of(dev * tok, tok), tok)

    def piece(dev, n):
        col = n * TILE
        if not isinstance(col, int):
            col = pl.multiple_of(col, TILE)
        return h_all.at[rows_of(dev), pl.ds(col, TILE)]

    def o_tile(n, carry):
        slot = lax.rem(kv_tiles + n, SLOTS)
        w_copy(wo, 0, slot).wait()
        y = jnp.dot(o_s[...], wbuf[slot], preferred_element_type=jnp.float32)
        x = xb[:, pl.ds(pl.multiple_of(n * TILE, TILE), TILE)].astype(jnp.float32)
        h_s[n] = (x + y).astype(jnp.bfloat16)
        remote(h_s.at[n], piece(me, n), h_send.at[0], hr_l.at[n], right).start()
        remote(h_s.at[n], piece(me, n), h_send.at[1], hr_r.at[n], left).start()
        remote(h_s.at[n], piece(me, n), h_send.at[2], hr_p.at[0], partner).start()
        pltpu.make_async_copy(h_s.at[n], piece(me, n), x_sem).start()
        return carry

    lax.fori_loop(0, o_tiles, o_tile, 0)

    half = o_tiles // 2
    for n in range(o_tiles):
        got(piece(left, n), hr_l.at[n])
        if n < half:
            remote(piece(left, n), piece(left, n), h_send.at[6], hr_o.at[n], right).start()
        remote(piece(left, n), piece(left, n), h_send.at[5], hr_p.at[3], partner).start()
        got(piece(right, n), hr_r.at[n])
        if n >= half:
            remote(piece(right, n), piece(right, n), h_send.at[7], hr_o.at[n], left).start()
        remote(piece(right, n), piece(right, n), h_send.at[3], hr_p.at[1], partner).start()
    for i in range(half):
        for n in (i, half + i):
            got(piece(opp, n), hr_o.at[n])
            remote(piece(opp, n), piece(opp, n), h_send.at[4], hr_p.at[2], partner).start()

    mine = h_all.at[rows_of(me)]
    got(mine, x_sem)
    for i in range(6):
        got(mine, h_send.at[i])
    half_cols = pl.ds(0, half * TILE)
    for i in (6, 7):
        got(h_all.at[rows_of(me), half_cols], h_send.at[i])
    for r in range(4):
        src = lax.rem(partner + 2 * r, group)
        got(h_all.at[rows_of(src)], hr_p.at[r])
    for i in range(6):
        got(kv.at[0, :, :, own, :], k_send.at[i])
    for i in (6, 7):
        got(kv.at[0, pl.ds(0, k_tiles), :, own, :], k_send.at[i])
    loc.wait()
    for d in range(1, group):
        got(meta_s, m_send.at[d - 1])
        got(meta_all.at[lax.rem(me + group - d, group)], m_recv.at[d - 1])


def dispatch_kernel(n_exp, own_exp, meta_ref, h_ref, hid_hbm, out_ref, hid_sem):
    s = pl.program_id(0)
    e = pl.program_id(1)
    me = lax.axis_index("sp")
    tok, width = h_ref.shape
    hid_copy = pltpu.make_async_copy(h_ref, hid_hbm, hid_sem)

    @pl.when((s == me) & (e == 0))
    def _():
        hid_copy.start()

    expert = me * own_exp + e
    slot = meta_ref[s, pl.ds(expert, 1), :]
    gate = meta_ref[s, pl.ds(n_exp + expert, 1), :]
    row = lax.broadcasted_iota(jnp.int32, (tok, tok), 0).astype(jnp.float32)
    pick = row == slot
    gate_col = jnp.sum(jnp.where(pick, gate, 0.0), axis=1, keepdims=True)
    pick = pick.astype(jnp.float32).astype(jnp.bfloat16)
    for c in range(0, width, TILE):
        got = jnp.dot(pick, h_ref[:, c:c + TILE], preferred_element_type=jnp.float32)
        out_ref[0, :, c:c + TILE] = (got * gate_col).astype(jnp.bfloat16)

    @pl.when((s == me) & (e == own_exp - 1))
    def _():
        hid_copy.wait()


def solution(mesh):
    group = mesh.shape['sp']
    row_spec = P(('dp', 'sp'), None)
    buf_spec = P(('dp', 'sp'), None, None)

    def device_step(x_loc, w_q, w_k, w_v, w_o, ids_loc, probs_loc):
        tok, width = x_loc.shape
        n_exp = probs_loc.shape[1]
        own_exp = n_exp // group
        seq = tok * group
        q_tiles = w_q.shape[1] // TILE
        kv_tiles = 2 * w_k.shape[1] // TILE
        o_tiles = width // TILE
        bf16 = jnp.bfloat16
        any_spec = pl.BlockSpec(memory_space=pl.ANY)
        vmem_spec = pl.BlockSpec(memory_space=pltpu.VMEM)
        dma = pltpu.SemaphoreType.DMA
        h_all, meta_all = pl.pallas_call(
            functools.partial(block_kernel, group, n_exp),
            out_shape=(jax.ShapeDtypeStruct((seq, width), bf16),
                       jax.ShapeDtypeStruct((group, 2 * n_exp, tok), jnp.float32)),
            in_specs=[any_spec] * 5 + [vmem_spec] * 2,
            out_specs=(any_spec, any_spec),
            scratch_shapes=[
                pltpu.VMEM((tok, width), bf16),
                pltpu.VMEM((SLOTS, width, TILE), bf16),
                pltpu.VMEM((4, kv_tiles, PER_TILE, 2 * tok, HEAD), bf16),
                pltpu.VMEM((q_tiles, PER_TILE * tok, HEAD), bf16),
                pltpu.VMEM((q_tiles, PER_TILE * tok, HEAD), jnp.float32),
                pltpu.VMEM((q_tiles, PER_TILE * tok, HEAD), jnp.float32),
                pltpu.VMEM((tok, q_tiles * TILE), bf16),
                pltpu.VMEM((o_tiles, tok, TILE), bf16),
                pltpu.VMEM((2 * n_exp, tok), jnp.float32),
                dma, dma((SLOTS,)),
                dma((8,)), dma((kv_tiles,)), dma((kv_tiles,)), dma((kv_tiles,)), dma((4,)),
                dma((8,)), dma((o_tiles,)), dma((o_tiles,)), dma((o_tiles,)), dma((4,)),
                dma((group - 1,)), dma((group - 1,)), dma,
            ],
            compiler_params=pltpu.CompilerParams(collective_id=0, has_side_effects=True,
                                                 vmem_limit_bytes=VMEM_LIMIT),
            name="block",
        )(x_loc, w_q, w_k, w_v, w_o, ids_loc, probs_loc)

        hidden_out, buf = pl.pallas_call(
            functools.partial(dispatch_kernel, n_exp, own_exp),
            out_shape=(jax.ShapeDtypeStruct((tok, width), bf16),
                       jax.ShapeDtypeStruct((own_exp, seq, width), bf16)),
            grid=(group, own_exp),
            in_specs=[pl.BlockSpec((group, 2 * n_exp, tok), lambda s, e: (0, 0, 0)),
                      pl.BlockSpec((tok, width), lambda s, e: (s, 0))],
            out_specs=(any_spec, pl.BlockSpec((1, tok, width), lambda s, e: (e, s, 0))),
            scratch_shapes=[dma],
            compiler_params=pltpu.CompilerParams(dimension_semantics=("arbitrary", "arbitrary")),
            name="dispatch",
        )(meta_all, h_all)
        return hidden_out, buf

    return jax.shard_map(device_step, mesh=mesh,
                         in_specs=(row_spec, P(), P(), P(), P(), row_spec, row_spec),
                         out_specs=(row_spec, buf_spec), check_vma=False)
```

time: 762 us -> 210 us (0.28)
  blocking collectives: 375 us -> 0 us
  Pallas kernels: 0 us -> 206 us
  local copies, waits for them, and re-layouts: 200 us -> 2.95 us
  matrix products: 99.1 us -> 0 us
  other arithmetic: 33.3 us -> 0 us
  waiting for transfers between devices: 30.8 us -> 0 us
  starting transfers between devices: 20.1 us -> 0 us
    all_to_all x1 -> x0, blocking collectives: 375 us -> none  [device_step(): recv_buf = lax.all_to_all(send_buf, 'sp', 0, 1, tiled=True)]
    pallas_call x0 -> x2, Pallas kernels: none -> 206 us  [the longest x1 174 us: device_step(): pl.pallas_call(functools.partial(block_kernel, group, n_exp), out_shape=(...]
    scatter x1 -> x0, local copies, waits for them, and re-layouts: 137 us -> none  [route_rows(): return send_buf.at[expert_ids, slot_rank].set(gated, unique_indices=True)]
    dot_general x6 -> x0, matrix products: 99.1 us -> none  [the longest x1 28.1 us: device_step(): jnp.einsum('gmqk,kgd->qgmd', weights, v_seq, preferred_element_type=jnp.f...]
    all_to_all x4 -> x0, waiting for transfers between devices: 30.8 us -> none  [the longest x1 15.2 us: device_step(): lax.all_to_all(attn_seq, 'sp', 0, 1, tiled=True)]
    all_to_all x4 -> x0, local copies, waits for them, and re-layouts: 28.8 us -> none  [the longest x1 22.9 us: device_step(): recv_buf = lax.all_to_all(send_buf, 'sp', 0, 1, tiled=True)]
    reduce_sum x3 -> x0, other arithmetic: 23 us -> none  [the longest x1 22.9 us: device_step(): jax.nn.softmax(jnp.where(causal, scores, -1e+30), axis=-1)]
    all_to_all x4 -> x0, starting transfers between devices: 20.1 us -> none  [the longest x1 6.01 us: device_step(): q_seq = lax.all_to_all(q_loc, 'sp', 1, 0, tiled=True)]
  transfers between devices with their start and end apart: 4 -> 0, of which waited for: 3 -> 0; matrix products, arithmetic and copies ran while one was open for 10% -> 0% of each run, Pallas kernels for 0% -> 0%
where the time goes in v1:
time: 210 us; the launch traced here: 209 us
  Pallas kernels  206 us (98%)
  local copies, waits for them, and re-layouts  2.95 us (1%)
    pallas_call x1, Pallas kernels, device_step(): pl.pallas_call(functools.partial(block_kernel, group, n_exp), out_shape=(...  174 us
    pallas_call x1, Pallas kernels, device_step(): pl.pallas_call(functools.partial(dispatch_kernel, n_exp, own_exp), out_sh...  31.4 us

profile of v1, /device:TPU:81, one launch (start us, length us, event | category | flops | bytes accessed | tf_op | source)
XLA Modules:
  0.0 209.4 jit_solution(14246862324589931862)
XLA Ops:
  0.6 1.5 copy.9.ids_ref
  2.1 1.5 copy.10.probs_ref
  3.6 174.4 %block.1 = (bf16[2048,4096]{1,0:T(8,128)(2,1)}, f32[8,32,256]{2,1,0:T(8,128)}) custom-call(bf16[256,4096]{1,0:T(8,128)(2,1)} %x_hbm.1, bf16[4096,4096]{1,0:T(8,128)(2,1)} %wq.1, bf16[4096,1024]{1,0:T(8,128)(2,1)} %wk.1, bf16[4096,1024]{1,0:T(8,128)(2,1)} %wv.1, bf16[4096,4096]{1,0:T(8,128)(2,1)} %wo.1, s32[256,2]{1,0:T(8,128)} %copy.9.ids_ref, ...), custom_call_target="tpu_custom_call" | custom-call | tf_op jit(solution)/shard_map/block/pallas_call | solution.py:307
  178.0 31.4 %dispatch.1 = (bf16[256,4096]{1,0:T(8,128)(2,1)}, bf16[2,2048,4096]{2,1,0:T(8,128)(2,1)}) custom-call(f32[8,32,256]{2,1,0:T(8,128)} %get-tuple-element.4.meta_ref, bf16[2048,4096]{1,0:T(8,128)(2,1)} %get-tuple-element.5.h_ref), custom_call_target="tpu_custom_call" | custom-call | tf_op jit(solution)/shard_map/dispatch/pallas_call | solution.py:333

commit v2 on v1

v2 whole, which is shorter than its diff:
```python
import functools
import math

import jax
import jax.numpy as jnp
from jax import lax
from jax.experimental import pallas as pl
from jax.experimental.pallas import tpu as pltpu
from jax.sharding import PartitionSpec as P

HEAD = 128
EXP2_SCALE = math.log2(math.e) / math.sqrt(HEAD)
MESH = pl.DeviceIdType.MESH
TILE = 512
SLOTS = 8
PER_TILE = TILE // HEAD
VMEM_LIMIT = 67_000_000
OUT_SLOTS = 10


def block_kernel(group, n_exp, x_hbm, wq, wk, wv, wo, ids_ref, probs_ref, h_all, meta_all,
                 xb, wbuf, kb, vb, q_s, acc, top_s, mass_s, keep_s, s_b, e_b, o_s, h_s, meta_s,
                 x_sem, w_sem, k_send, kr_l, kr_r, kr_o, kr_p, h_send, hr_l, hr_r, hr_o, hr_p, m_send, m_recv, m_loc):
    tok = xb.shape[0]
    chips = group // 2
    q_tiles = wq.shape[1] // TILE
    k_tiles = wk.shape[1] // TILE
    kv_tiles = 2 * k_tiles
    o_tiles = wo.shape[1] // TILE
    me = lax.axis_index("sp")
    core = lax.rem(me, 2)
    chip = lax.div(me, 2)
    right = lax.rem(me + 2, group)
    left = lax.rem(me + group - 2, group)
    partner = me + 1 - 2 * core
    opp = lax.rem(me + 4, group)
    last = chips - 1

    def remote(src, dst, send, recv, dev):
        return pltpu.make_async_remote_copy(src_ref=src, dst_ref=dst, send_sem=send, recv_sem=recv,
                                            device_id={"sp": dev}, device_id_type=MESH)

    def got(ref, sem):
        pltpu.make_async_copy(ref, ref, sem).wait()

    def w_copy(arr, col, slot):
        if not isinstance(col, int):
            col = pl.multiple_of(col, TILE)
        return pltpu.make_async_copy(arr.at[:, pl.ds(col, TILE)], wbuf.at[slot], w_sem.at[slot])

    x_copy = pltpu.make_async_copy(x_hbm, xb, x_sem)
    x_copy.start()
    for p in range(SLOTS):
        if p < k_tiles:
            w_copy(wk, p * TILE, p).start()
        elif p < kv_tiles:
            w_copy(wv, (p - k_tiles) * TILE, p).start()
        else:
            w_copy(wq, (p - kv_tiles) * TILE, p).start()

    barrier = pltpu.get_barrier_semaphore()
    for d in range(1, group):
        pl.semaphore_signal(barrier, inc=1, device_id={"sp": lax.rem(me + d, group)}, device_id_type=MESH)
    x_copy.wait()

    sends_right = chip < last
    sends_left_k = chip == 0
    sends_left_v = chip < 2
    gets_left = chip > 0
    gets_right_k = chip == last
    gets_right_v = (chip == last) | (chip == 0)
    fwd_k = (chip > 0) & (chip < last)
    fwd_v = (chip == last) | (chip == 0)
    gets_opp = chip >= 2

    def k_tile(p, carry):
        w_copy(wk, 0, p).wait()
        y = jnp.dot(xb[...], wbuf[p], preferred_element_type=jnp.float32).astype(jnp.bfloat16)
        for h in range(PER_TILE):
            kb[0, 0, p, h] = y[:, h * HEAD:(h + 1) * HEAD]
        w_copy(wq, (SLOTS - kv_tiles + p) * TILE, p).start()

        @pl.when(p == 0)
        def _():
            pl.semaphore_wait(barrier, group - 1)

        src = kb.at[0, 0, p]

        @pl.when(sends_right)
        def _():
            remote(src, kb.at[3, 0, p], k_send.at[0], kr_l.at[p], right).start()

        @pl.when(sends_left_k)
        def _():
            remote(src, kb.at[1, 0, p], k_send.at[1], kr_r.at[p], left).start()

        @pl.when(core == 0)
        def _():
            remote(src, kb.at[0, 1, p], k_send.at[2], kr_p.at[0], partner).start()

        return carry

    lax.fori_loop(0, k_tiles, k_tile, 0)

    def v_tile(p, carry):
        w_copy(wv, 0, k_tiles + p).wait()
        y = jnp.dot(xb[...], wbuf[k_tiles + p], preferred_element_type=jnp.float32)
        for h in range(PER_TILE):
            vb[0, 0, p, h] = jnp.transpose(y[:, h * HEAD:(h + 1) * HEAD]).astype(jnp.bfloat16)
        w_copy(wq, (SLOTS - k_tiles + p) * TILE, k_tiles + p).start()
        src = vb.at[0, 0, p]

        @pl.when(sends_right)
        def _():
            remote(src, vb.at[3, 0, p], k_send.at[3], kr_l.at[k_tiles + p], right).start()

        @pl.when(sends_left_v)
        def _():
            remote(src, vb.at[1, 0, p], k_send.at[4], kr_r.at[k_tiles + p], left).start()

        @pl.when(core == 0)
        def _():
            remote(src, vb.at[0, 1, p], k_send.at[5], kr_p.at[4], partner).start()

        return carry

    lax.fori_loop(0, k_tiles, v_tile, 0)

    def q_tile(n, carry):
        slot = lax.rem(kv_tiles + n, SLOTS)
        w_copy(wq, 0, slot).wait()
        y = jnp.dot(xb[...], wbuf[slot], preferred_element_type=jnp.float32).astype(jnp.bfloat16)
        for h in range(PER_TILE):
            q_s[n, h] = y[:, h * HEAD:(h + 1) * HEAD]
        w_copy(wo, n * TILE, slot).start()
        return carry

    lax.fori_loop(0, q_tiles, q_tile, 0)

    def k_partner(r, p):
        remote(kb.at[r, 0, p], kb.at[r, 1, p], k_send.at[5 + r], kr_p.at[r], partner).start()

    def v_partner(r, p):
        remote(vb.at[r, 0, p], vb.at[r, 1, p], k_send.at[8 + r], kr_p.at[4 + r], partner).start()

    @pl.when(gets_left)
    def _():
        for p in range(k_tiles):
            got(kb.at[3, 0, p], kr_l.at[p])

            @pl.when(fwd_k)
            def _():
                remote(kb.at[3, 0, p], kb.at[2, 0, p], k_send.at[12], kr_o.at[p], right).start()

            k_partner(3, p)

    expert = lax.broadcasted_iota(jnp.int32, (n_exp, tok), 0)
    hit0 = expert == ids_ref[0:1, :]
    hit1 = expert == ids_ref[1:2, :]
    probs = probs_ref[...]
    p0 = jnp.sum(jnp.where(hit0, probs, 0.0), axis=0, keepdims=True)
    p1 = jnp.sum(jnp.where(hit1, probs, 0.0), axis=0, keepdims=True)
    total = p0 + p1
    hits = hit0 | hit1
    before = (lax.broadcasted_iota(jnp.int32, (tok, tok), 0)
              < lax.broadcasted_iota(jnp.int32, (tok, tok), 1)).astype(jnp.float32).astype(jnp.bfloat16)
    earlier = jnp.dot(hits.astype(jnp.float32).astype(jnp.bfloat16), before, preferred_element_type=jnp.float32)
    meta_s[0:n_exp, :] = jnp.where(hits, earlier, -1.0)
    meta_s[n_exp:2 * n_exp, :] = jnp.where(hit0, p0 / total, jnp.where(hit1, p1 / total, 0.0))

    def attend(r, parts, first=False, diagonal=False):
        keys = parts * tok
        every = pl.ds(0, keys)
        if diagonal:
            key_i = lax.broadcasted_iota(jnp.int32, (tok, tok), 0)
            row_i = lax.broadcasted_iota(jnp.int32, (tok, tok), 1)
            seen = row_i >= key_i

        def score(g, h):
            kp = lax.div(g, PER_TILE)
            kh = lax.rem(g, PER_TILE)
            q = q_s[g, h]
            top = None if first else top_s[g, h]
            old = top
            for o in range(parts):
                s = lax.dot_general(kb[r, o, kp, kh], q, (((1,), (1,)), ((), ())), preferred_element_type=jnp.float32)
                if diagonal and o == 0:
                    s = jnp.where(seen, s, -1e30)
                s_b[h % 2, o] = s
                high = jnp.max(s, axis=0, keepdims=True)
                top = high if top is None else jnp.maximum(top, high)
            top_s[g, h] = top
            if not first:
                keep_s[h] = jnp.exp2((old - top) * EXP2_SCALE)

        def weigh(g, h):
            top = top_s[g, h]
            mass = None
            for o in range(parts):
                e = jnp.exp2((s_b[h % 2, o] - top) * EXP2_SCALE)
                e_b[h % 2, o * tok:(o + 1) * tok, :] = e.astype(jnp.bfloat16)
                part = jnp.sum(e, axis=0, keepdims=True)
                mass = part if mass is None else mass + part
            mass_s[g, h] = mass if first else mass + keep_s[h] * mass_s[g, h]

        def apply(g, h, into):
            kp = lax.div(g, PER_TILE)
            kh = lax.rem(g, PER_TILE)
            v = jnp.concatenate([vb[r, o, kp, kh] for o in range(parts)], axis=1)
            out = jnp.dot(v, e_b[h % 2, every, :], preferred_element_type=jnp.float32)
            acc[into, h] = out if first else out + keep_s[h] * acc[into, h]

        last_h = PER_TILE - 1

        def head_group(g, carry):
            below = jnp.maximum(g - 1, 0)
            into = lax.select(g == 0, q_tiles, g - 1)
            above = jnp.minimum(g + 1, q_tiles - 1)
            for h in range(PER_TILE):
                if h < last_h:
                    score(g, h + 1)
                else:
                    score(above, 0)
                weigh(g, h)
                if h > 0:
                    apply(g, h - 1, g)
                else:
                    apply(below, last_h, into)
            return carry

        score(0, 0)
        lax.fori_loop(0, q_tiles, head_group, 0)
        apply(q_tiles - 1, last_h, q_tiles - 1)

    acc[q_tiles, PER_TILE - 1] = jnp.zeros((HEAD, tok), jnp.float32)
    e_b[(PER_TILE - 1) % 2] = jnp.zeros((2 * tok, tok), jnp.bfloat16)
    keep_s[PER_TILE - 1] = jnp.zeros((1, tok), jnp.float32)

    @pl.when(core == 0)
    def _():
        attend(0, 1, first=True, diagonal=True)

    @pl.when(core == 1)
    def _():
        got(kb.at[0, 1], kr_p.at[0])
        got(vb.at[0, 1], kr_p.at[4])
        attend(0, 2, first=True, diagonal=True)

    m_rows = meta_all.at[me]
    loc = pltpu.make_async_copy(meta_s, m_rows, m_loc)
    loc.start()
    for d in range(1, group):
        remote(meta_s, m_rows, m_send.at[d - 1], m_recv.at[d - 1], lax.rem(me + d, group)).start()

    @pl.when(gets_right_v)
    def _():
        for p in range(k_tiles):
            got(vb.at[1, 0, p], kr_r.at[k_tiles + p])
            remote(vb.at[1, 0, p], vb.at[2, 0, p], k_send.at[13], kr_o.at[k_tiles + p], left).start()

    @pl.when(gets_right_k)
    def _():
        for p in range(k_tiles):
            got(kb.at[1, 0, p], kr_r.at[p])
            k_partner(1, p)
            v_partner(1, p)

    @pl.when(gets_left)
    def _():
        for p in range(k_tiles):
            got(vb.at[3, 0, p], kr_l.at[k_tiles + p])
            v_partner(3, p)
        got(kb.at[3, 1], kr_p.at[3])
        got(vb.at[3, 1], kr_p.at[7])
        attend(3, 2)

    @pl.when(gets_right_k)
    def _():
        got(kb.at[1, 1], kr_p.at[1])
        got(vb.at[1, 1], kr_p.at[5])
        attend(1, 2)

    @pl.when(gets_opp)
    def _():
        for p in range(k_tiles):
            got(kb.at[2, 0, p], kr_o.at[p])
            k_partner(2, p)
            got(vb.at[2, 0, p], kr_o.at[k_tiles + p])
            v_partner(2, p)
        got(kb.at[2, 1], kr_p.at[2])
        got(vb.at[2, 1], kr_p.at[6])
        attend(2, 2)

    def finish(g, carry):
        for h in range(PER_TILE):
            o = jnp.transpose(acc[g, h] * (1.0 / mass_s[g, h]))
            o_s[:, pl.ds(pl.multiple_of(g * TILE + h * HEAD, HEAD), HEAD)] = o.astype(jnp.bfloat16)
        return carry

    lax.fori_loop(0, q_tiles, finish, 0)

    def rows_of(dev):
        return pl.ds(pl.multiple_of(dev * tok, tok), tok)

    def piece(dev, n):
        col = n * TILE
        if not isinstance(col, int):
            col = pl.multiple_of(col, TILE)
        return h_all.at[rows_of(dev), pl.ds(col, TILE)]

    def o_tile(n, carry):
        slot = lax.rem(kv_tiles + n, SLOTS)
        w_copy(wo, 0, slot).wait()
        y = jnp.dot(o_s[...], wbuf[slot], preferred_element_type=jnp.float32)
        x = xb[:, pl.ds(pl.multiple_of(n * TILE, TILE), TILE)].astype(jnp.float32)
        h_s[n] = (x + y).astype(jnp.bfloat16)
        remote(h_s.at[n], piece(me, n), h_send.at[0], hr_l.at[n], right).start()
        remote(h_s.at[n], piece(me, n), h_send.at[1], hr_r.at[n], left).start()
        remote(h_s.at[n], piece(me, n), h_send.at[2], hr_p.at[0], partner).start()
        pltpu.make_async_copy(h_s.at[n], piece(me, n), x_sem).start()
        return carry

    lax.fori_loop(0, o_tiles, o_tile, 0)

    def from_left():
        for n in range(o_tiles):
            got(piece(left, n), hr_l.at[n])
            if n % 2 == 0:
                remote(piece(left, n), piece(left, n), h_send.at[6], hr_o.at[n], right).start()
            remote(piece(left, n), piece(left, n), h_send.at[5], hr_p.at[3], partner).start()

    def from_right():
        for n in range(o_tiles):
            got(piece(right, n), hr_r.at[n])
            if n % 2 == 1:
                remote(piece(right, n), piece(right, n), h_send.at[7], hr_o.at[n], left).start()
            remote(piece(right, n), piece(right, n), h_send.at[3], hr_p.at[1], partner).start()

    early_right = (chip == 0) | (chip == last)

    @pl.when(early_right)
    def _():
        from_right()
        from_left()

    @pl.when(jnp.logical_not(early_right))
    def _():
        from_left()
        from_right()

    for n in range(o_tiles):
        got(piece(opp, n), hr_o.at[n])
        remote(piece(opp, n), piece(opp, n), h_send.at[4], hr_p.at[2], partner).start()

    mine = h_all.at[rows_of(me)]
    got(mine, x_sem)
    for i in range(6):
        got(mine, h_send.at[i])
    for i in (6, 7):
        got(h_all.at[rows_of(me), pl.ds(0, o_tiles // 2 * TILE)], h_send.at[i])
    for r in range(chips):
        got(h_all.at[rows_of(lax.rem(partner + 2 * r, group))], hr_p.at[r])
    k_own = kb.at[0, 0]
    v_own = vb.at[0, 0]
    for when, waits in ((sends_right, ((k_own, 0), (v_own, 3))), (sends_left_k, ((k_own, 1),)), (sends_left_v, ((v_own, 4),)),
                        (core == 0, ((k_own, 2), (v_own, 5))), (gets_left, ((k_own, 8), (v_own, 11))),
                        (gets_right_k, ((k_own, 6), (v_own, 9))), (gets_opp, ((k_own, 7), (v_own, 10))),
                        (fwd_k, ((k_own, 12),)), (fwd_v, ((v_own, 13),))):
        @pl.when(when)
        def _(waits=waits):
            for ref, i in waits:
                got(ref, k_send.at[i])

    loc.wait()
    for d in range(1, group):
        got(meta_s, m_send.at[d - 1])
        got(meta_all.at[lax.rem(me + group - d, group)], m_recv.at[d - 1])


def dispatch_kernel(n_exp, own_exp, meta_ref, h_hbm, hid_hbm, buf_hbm, hb, ob, h_sem, o_sem, hid_sem):
    group, tok, width = hb.shape
    slots = ob.shape[0]
    me = lax.axis_index("sp")
    steps = group * own_exp
    row = lax.broadcasted_iota(jnp.int32, (tok, tok), 0).astype(jnp.float32)

    def h_copy(s):
        return pltpu.make_async_copy(h_hbm.at[pl.ds(s * tok, tok)], hb.at[s], h_sem.at[s])

    def o_copy(i):
        s = lax.div(i, own_exp)
        return pltpu.make_async_copy(ob.at[lax.rem(i, slots)],
                                     buf_hbm.at[lax.rem(i, own_exp), pl.ds(pl.multiple_of(s * tok, tok), tok)],
                                     o_sem.at[lax.rem(i, slots)])

    for s in range(group):
        h_copy(s).start()

    def step(i, carry):
        s = lax.div(i, own_exp)
        e = lax.rem(i, own_exp)

        @pl.when(e == 0)
        def _():
            pltpu.make_async_copy(hb.at[s], hb.at[s], h_sem.at[s]).wait()

            @pl.when(s == me)
            def _():
                pltpu.make_async_copy(hb.at[s], hid_hbm, hid_sem).start()

        @pl.when(i >= slots)
        def _():
            o_copy(i - slots).wait()

        expert = me * own_exp + e
        slot = meta_ref[s, pl.ds(expert, 1), :]
        gate = meta_ref[s, pl.ds(n_exp + expert, 1), :]
        pick = row == slot
        gate_col = jnp.sum(jnp.where(pick, gate, 0.0), axis=1, keepdims=True)
        pick = pick.astype(jnp.float32).astype(jnp.bfloat16)
        o = lax.rem(i, slots)
        for c in range(0, width, TILE):
            rows = jnp.dot(pick, hb[s, :, c:c + TILE], preferred_element_type=jnp.float32)
            ob[o, :, c:c + TILE] = (rows * gate_col).astype(jnp.bfloat16)
        o_copy(i).start()
        return carry

    lax.fori_loop(0, steps, step, 0)
    for i in range(steps - slots, steps):
        o_copy(i).wait()
    pltpu.make_async_copy(hb.at[0], hid_hbm, hid_sem).wait()


def solution(mesh):
    group = mesh.shape['sp']
    row_spec = P(('dp', 'sp'), None)
    buf_spec = P(('dp', 'sp'), None, None)

    def device_step(x_loc, w_q, w_k, w_v, w_o, ids_loc, probs_loc):
        tok, width = x_loc.shape
        n_exp = probs_loc.shape[1]
        own_exp = n_exp // group
        seq = tok * group
        q_tiles = w_q.shape[1] // TILE
        k_tiles = w_k.shape[1] // TILE
        chips = group // 2
        o_tiles = width // TILE
        bf16 = jnp.bfloat16
        any_spec = pl.BlockSpec(memory_space=pl.ANY)
        vmem_spec = pl.BlockSpec(memory_space=pltpu.VMEM)
        dma = pltpu.SemaphoreType.DMA
        h_all, meta_all = pl.pallas_call(
            functools.partial(block_kernel, group, n_exp),
            out_shape=(jax.ShapeDtypeStruct((seq, width), bf16),
                       jax.ShapeDtypeStruct((group, 2 * n_exp, tok), jnp.float32)),
            in_specs=[any_spec] * 5 + [vmem_spec] * 2,
            out_specs=(any_spec, any_spec),
            scratch_shapes=[
                pltpu.VMEM((tok, width), bf16),
                pltpu.VMEM((SLOTS, width, TILE), bf16),
                pltpu.VMEM((chips, 2, k_tiles, PER_TILE, tok, HEAD), bf16),
                pltpu.VMEM((chips, 2, k_tiles, PER_TILE, HEAD, tok), bf16),
                pltpu.VMEM((q_tiles, PER_TILE, tok, HEAD), bf16),
                pltpu.VMEM((q_tiles + 1, PER_TILE, HEAD, tok), jnp.float32),
                pltpu.VMEM((q_tiles, PER_TILE, 1, tok), jnp.float32),
                pltpu.VMEM((q_tiles, PER_TILE, 1, tok), jnp.float32),
                pltpu.VMEM((PER_TILE, 1, tok), jnp.float32),
                pltpu.VMEM((2, 2, tok, tok), jnp.float32),
                pltpu.VMEM((2, 2 * tok, tok), bf16),
                pltpu.VMEM((tok, q_tiles * TILE), bf16),
                pltpu.VMEM((o_tiles, tok, TILE), bf16),
                pltpu.VMEM((2 * n_exp, tok), jnp.float32),
                dma, dma((SLOTS,)),
                dma((14,)), dma((2 * k_tiles,)), dma((2 * k_tiles,)), dma((2 * k_tiles,)), dma((2 * chips,)),
                dma((8,)), dma((o_tiles,)), dma((o_tiles,)), dma((o_tiles,)), dma((chips,)),
                dma((group - 1,)), dma((group - 1,)), dma,
            ],
            compiler_params=pltpu.CompilerParams(collective_id=0, has_side_effects=True,
                                                 vmem_limit_bytes=VMEM_LIMIT),
            name="block",
        )(x_loc, w_q, w_k, w_v, w_o, ids_loc.T, probs_loc.T)

        hidden_out, buf = pl.pallas_call(
            functools.partial(dispatch_kernel, n_exp, own_exp),
            out_shape=(jax.ShapeDtypeStruct((tok, width), bf16),
                       jax.ShapeDtypeStruct((own_exp, seq, width), bf16)),
            in_specs=[vmem_spec, any_spec],
            out_specs=(any_spec, any_spec),
            scratch_shapes=[pltpu.VMEM((group, tok, width), bf16), pltpu.VMEM((OUT_SLOTS, tok, width), bf16),
                            dma((group,)), dma((OUT_SLOTS,)), dma],
            compiler_params=pltpu.CompilerParams(vmem_limit_bytes=VMEM_LIMIT),
            name="dispatch",
        )(meta_all, h_all)
        return hidden_out, buf

    return jax.shard_map(device_step, mesh=mesh,
                         in_specs=(row_spec, P(), P(), P(), P(), row_spec, row_spec),
                         out_specs=(row_spec, buf_spec), check_vma=False)
```

time: 210 us -> 159 us (0.76)
  Pallas kernels: 206 us -> 158 us
  local copies, waits for them, and re-layouts: 2.95 us -> 0 us
    pallas_call x1, Pallas kernels: 174 us -> 141 us  [device_step(): pl.pallas_call(functools.partial(block_kernel, group, n_exp), out_shape=(...]
    pallas_call x1, Pallas kernels: 31.4 us -> 17.4 us  [device_step(): pl.pallas_call(functools.partial(dispatch_kernel, n_exp, own_exp), out_sh...]
    unnamed x2 -> x0, local copies, waits for them, and re-layouts: 2.95 us -> none
where the time goes in v2:
time: 159 us
  Pallas kernels  158 us (99%)
    pallas_call x1, Pallas kernels, device_step(): pl.pallas_call(functools.partial(block_kernel, group, n_exp), out_shape=(...  141 us
    pallas_call x1, Pallas kernels, device_step(): pl.pallas_call(functools.partial(dispatch_kernel, n_exp, own_exp), out_sh...  17.4 us

profile of v2, /device:TPU:81, one launch (start us, length us, event | category | flops | bytes accessed | tf_op | source)
XLA Modules:
  0.0 159.1 jit_solution(2504776075575888397)
XLA Ops:
  0.6 141.1 %block.1 = (bf16[2048,4096]{1,0:T(8,128)(2,1)}, f32[8,32,256]{2,1,0:T(8,128)}) custom-call(bf16[256,4096]{1,0:T(8,128)(2,1)} %x_hbm.1, bf16[4096,4096]{1,0:T(8,128)(2,1)} %wq.1, bf16[4096,1024]{1,0:T(8,128)(2,1)} %wk.1, bf16[4096,1024]{1,0:T(8,128)(2,1)} %wv.1, bf16[4096,4096]{1,0:T(8,128)(2,1)} %wo.1, s32[2,256]{1,0:T(2,128)} %bitcast.3, f32[16,256]{1,0:T(8,128)} %bitcast.2), custom_call_target="tpu_custom_call" | custom-call | tf_op jit(solution)/shard_map/block/pallas_call | solution.py:452
  141.7 17.4 %dispatch.1 = (bf16[256,4096]{1,0:T(8,128)(2,1)}, bf16[2,2048,4096]{2,1,0:T(8,128)(2,1)}) custom-call(f32[8,32,256]{2,1,0:T(8,128)} %get-tuple-element.4.meta_ref, bf16[2048,4096]{1,0:T(8,128)(2,1)} %get-tuple-element.5.h_hbm), custom_call_target="tpu_custom_call" | custom-call | tf_op jit(solution)/shard_map/dispatch/pallas_call | solution.py:483

commit v3 on v2

--- a/solution.py
+++ b/solution.py
@@ -14,13 +14,14 @@
 TILE = 512
 SLOTS = 8
 PER_TILE = TILE // HEAD
+SEND_TILES = 2
 VMEM_LIMIT = 67_000_000
 OUT_SLOTS = 10
 
 
 def block_kernel(group, n_exp, x_hbm, wq, wk, wv, wo, ids_ref, probs_ref, h_all, meta_all,
-                 xb, wbuf, kb, vb, q_s, acc, top_s, mass_s, keep_s, s_b, e_b, o_s, h_s, meta_s,
-                 x_sem, w_sem, k_send, kr_l, kr_r, kr_o, kr_p, h_send, hr_l, hr_r, hr_o, hr_p, m_send, m_recv, m_loc):
+                 xb, wbuf, kb, vb, q_s, acc, top_s, mass_s, keep_s, s_b, e_b, o_s, h_s, land, meta_s,
+                 x_sem, w_sem, k_send, kr_l, kr_r, kr_o, kr_p, h_send, hr_l, hr_r, hr_o, hr_p, h_loc, m_send, m_recv, m_loc):
     tok = xb.shape[0]
     chips = group // 2
     q_tiles = wq.shape[1] // TILE
@@ -303,38 +304,46 @@
         return pl.ds(pl.multiple_of(dev * tok, tok), tok)
 
     def piece(dev, n):
-        col = n * TILE
+        col = n * cols
         if not isinstance(col, int):
-            col = pl.multiple_of(col, TILE)
-        return h_all.at[rows_of(dev), pl.ds(col, TILE)]
-
-    def o_tile(n, carry):
-        slot = lax.rem(kv_tiles + n, SLOTS)
-        w_copy(wo, 0, slot).wait()
-        y = jnp.dot(o_s[...], wbuf[slot], preferred_element_type=jnp.float32)
-        x = xb[:, pl.ds(pl.multiple_of(n * TILE, TILE), TILE)].astype(jnp.float32)
-        h_s[n] = (x + y).astype(jnp.bfloat16)
-        remote(h_s.at[n], piece(me, n), h_send.at[0], hr_l.at[n], right).start()
-        remote(h_s.at[n], piece(me, n), h_send.at[1], hr_r.at[n], left).start()
-        remote(h_s.at[n], piece(me, n), h_send.at[2], hr_p.at[0], partner).start()
-        pltpu.make_async_copy(h_s.at[n], piece(me, n), x_sem).start()
+            col = pl.multiple_of(col, cols)
+        return h_all.at[rows_of(dev), pl.ds(col, cols)]
+
+    cols = SEND_TILES * TILE
+    pieces = o_tiles // SEND_TILES
+
+    def keep(ref, dev, r, n):
+        pltpu.make_async_copy(ref, piece(dev, n), h_loc.at[r]).start()
+        remote(ref, piece(dev, n), h_send.at[2 + r], hr_p.at[r], partner).start()
+
+    def o_piece(n, carry):
+        for t in range(SEND_TILES):
+            tile = n * SEND_TILES + t
+            slot = lax.rem(kv_tiles + tile, SLOTS)
+            w_copy(wo, 0, slot).wait()
+            y = jnp.dot(o_s[...], wbuf[slot], preferred_element_type=jnp.float32)
+            x = xb[:, pl.ds(pl.multiple_of(tile * TILE, TILE), TILE)].astype(jnp.float32)
+            h_s[n, :, t * TILE:(t + 1) * TILE] = (x + y).astype(jnp.bfloat16)
+        remote(h_s.at[n], land.at[0, n], h_send.at[0], hr_l.at[n], right).start()
+        remote(h_s.at[n], land.at[1, n], h_send.at[1], hr_r.at[n], left).start()
+        keep(h_s.at[n], me, 0, n)
         return carry
 
-    lax.fori_loop(0, o_tiles, o_tile, 0)
+    lax.fori_loop(0, pieces, o_piece, 0)
 
     def from_left():
-        for n in range(o_tiles):
-            got(piece(left, n), hr_l.at[n])
+        for n in range(pieces):
+            got(land.at[0, n], hr_l.at[n])
             if n % 2 == 0:
-                remote(piece(left, n), piece(left, n), h_send.at[6], hr_o.at[n], right).start()
-            remote(piece(left, n), piece(left, n), h_send.at[5], hr_p.at[3], partner).start()
+                remote(land.at[0, n], land.at[2, n], h_send.at[6], hr_o.at[n], right).start()
+            keep(land.at[0, n], left, 3, n)
 
     def from_right():
-        for n in range(o_tiles):
-            got(piece(right, n), hr_r.at[n])
+        for n in range(pieces):
+            got(land.at[1, n], hr_r.at[n])
             if n % 2 == 1:
-                remote(piece(right, n), piece(right, n), h_send.at[7], hr_o.at[n], left).start()
-            remote(piece(right, n), piece(right, n), h_send.at[3], hr_p.at[1], partner).start()
+                remote(land.at[1, n], land.at[2, n], h_send.at[7], hr_o.at[n], left).start()
+            keep(land.at[1, n], right, 1, n)
 
     early_right = (chip == 0) | (chip == last)
 
@@ -348,16 +357,17 @@
         from_left()
         from_right()
 
-    for n in range(o_tiles):
-        got(piece(opp, n), hr_o.at[n])
-        remote(piece(opp, n), piece(opp, n), h_send.at[4], hr_p.at[2], partner).start()
+    for n in range(pieces):
+        got(land.at[2, n], hr_o.at[n])
+        keep(land.at[2, n], opp, 2, n)
 
     mine = h_all.at[rows_of(me)]
-    got(mine, x_sem)
     for i in range(6):
         got(mine, h_send.at[i])
     for i in (6, 7):
         got(h_all.at[rows_of(me), pl.ds(0, o_tiles // 2 * TILE)], h_send.at[i])
+    for r in range(chips):
+        got(h_all.at[rows_of(lax.rem(me + 2 * r, group))], h_loc.at[r])
     for r in range(chips):
         got(h_all.at[rows_of(lax.rem(partner + 2 * r, group))], hr_p.at[r])
     k_own = kb.at[0, 0]
@@ -444,7 +454,7 @@
         q_tiles = w_q.shape[1] // TILE
         k_tiles = w_k.shape[1] // TILE
         chips = group // 2
-        o_tiles = width // TILE
+        pieces = width // (SEND_TILES * TILE)
         bf16 = jnp.bfloat16
         any_spec = pl.BlockSpec(memory_space=pl.ANY)
         vmem_spec = pl.BlockSpec(memory_space=pltpu.VMEM)
@@ -468,11 +478,12 @@
                 pltpu.VMEM((2, 2, tok, tok), jnp.float32),
                 pltpu.VMEM((2, 2 * tok, tok), bf16),
                 pltpu.VMEM((tok, q_tiles * TILE), bf16),
-                pltpu.VMEM((o_tiles, tok, TILE), bf16),
+                pltpu.VMEM((pieces, tok, SEND_TILES * TILE), bf16),
+                pltpu.VMEM((3, pieces, tok, SEND_TILES * TILE), bf16),
                 pltpu.VMEM((2 * n_exp, tok), jnp.float32),
                 dma, dma((SLOTS,)),
                 dma((14,)), dma((2 * k_tiles,)), dma((2 * k_tiles,)), dma((2 * k_tiles,)), dma((2 * chips,)),
-                dma((8,)), dma((o_tiles,)), dma((o_tiles,)), dma((o_tiles,)), dma((chips,)),
+                dma((8,)), dma((pieces,)), dma((pieces,)), dma((pieces,)), dma((chips,)), dma((chips,)),
                 dma((group - 1,)), dma((group - 1,)), dma,
             ],
             compiler_params=pltpu.CompilerParams(collective_id=0, has_side_effects=True,

time: 159 us -> 161 us (1.013)
  Pallas kernels: 158 us -> 160 us
    pallas_call x1, Pallas kernels: 141 us -> 143 us  [device_step(): pl.pallas_call(functools.partial(block_kernel, group, n_exp), out_shape=(...]
where the time goes in v3:
time: 161 us
  Pallas kernels  160 us (99%)
    pallas_call x1, Pallas kernels, device_step(): pl.pallas_call(functools.partial(block_kernel, group, n_exp), out_shape=(...  143 us
    pallas_call x1, Pallas kernels, device_step(): pl.pallas_call(functools.partial(dispatch_kernel, n_exp, own_exp), out_sh...  17.4 us

profile of v3, /device:TPU:81, one launch (start us, length us, event | category | flops | bytes accessed | tf_op | source)
XLA Modules:
  0.0 161.0 jit_solution(11175859556058571227)
XLA Ops:
  0.6 143.0 %block.1 = (bf16[2048,4096]{1,0:T(8,128)(2,1)}, f32[8,32,256]{2,1,0:T(8,128)}) custom-call(bf16[256,4096]{1,0:T(8,128)(2,1)} %x_hbm.1, bf16[4096,4096]{1,0:T(8,128)(2,1)} %wq.1, bf16[4096,1024]{1,0:T(8,128)(2,1)} %wk.1, bf16[4096,1024]{1,0:T(8,128)(2,1)} %wv.1, bf16[4096,4096]{1,0:T(8,128)(2,1)} %wo.1, s32[2,256]{1,0:T(2,128)} %bitcast.3, f32[16,256]{1,0:T(8,128)} %bitcast.2), custom_call_target="tpu_custom_call" | custom-call | tf_op jit(solution)/shard_map/block/pallas_call | solution.py:462
  143.7 17.4 %dispatch.1 = (bf16[256,4096]{1,0:T(8,128)(2,1)}, bf16[2,2048,4096]{2,1,0:T(8,128)(2,1)}) custom-call(f32[8,32,256]{2,1,0:T(8,128)} %get-tuple-element.4.meta_ref, bf16[2048,4096]{1,0:T(8,128)(2,1)} %get-tuple-element.5.h_hbm), custom_call_target="tpu_custom_call" | custom-call | tf_op jit(solution)/shard_map/dispatch/pallas_call | solution.py:494

commit v4 on v2

--- a/solution.py
+++ b/solution.py
@@ -14,7 +14,9 @@
 TILE = 512
 SLOTS = 8
 PER_TILE = TILE // HEAD
+AHEAD = 3
 VMEM_LIMIT = 67_000_000
+VIA_NEXT = ((0, 2, 3, 5, 7), (0, 3, 6), (1, 4, 6), (0, 1, 3, 4, 6, 7))
 OUT_SLOTS = 10
 
 
@@ -50,18 +52,13 @@
 
     x_copy = pltpu.make_async_copy(x_hbm, xb, x_sem)
     x_copy.start()
-    for p in range(SLOTS):
-        if p < k_tiles:
-            w_copy(wk, p * TILE, p).start()
-        elif p < kv_tiles:
-            w_copy(wv, (p - k_tiles) * TILE, p).start()
-        else:
-            w_copy(wq, (p - kv_tiles) * TILE, p).start()
+    w_copy(wk, 0, 0).start()
 
     barrier = pltpu.get_barrier_semaphore()
     for d in range(1, group):
         pl.semaphore_signal(barrier, inc=1, device_id={"sp": lax.rem(me + d, group)}, device_id_type=MESH)
     x_copy.wait()
+    w_copy(wk, TILE, 1).start()
 
     sends_right = chip < last
     sends_left_k = chip == 0
@@ -75,10 +72,15 @@
 
     def k_tile(p, carry):
         w_copy(wk, 0, p).wait()
+        w_copy(wv, p * TILE, k_tiles + p).start()
+
+        @pl.when(p == k_tiles - 1)
+        def _():
+            w_copy(wq, 0, kv_tiles).start()
+
         y = jnp.dot(xb[...], wbuf[p], preferred_element_type=jnp.float32).astype(jnp.bfloat16)
         for h in range(PER_TILE):
             kb[0, 0, p, h] = y[:, h * HEAD:(h + 1) * HEAD]
-        w_copy(wq, (SLOTS - kv_tiles + p) * TILE, p).start()
 
         @pl.when(p == 0)
         def _():
@@ -104,10 +106,10 @@
 
     def v_tile(p, carry):
         w_copy(wv, 0, k_tiles + p).wait()
+        w_copy(wq, (1 + p) * TILE, kv_tiles + 1 + p).start()
         y = jnp.dot(xb[...], wbuf[k_tiles + p], preferred_element_type=jnp.float32)
         for h in range(PER_TILE):
             vb[0, 0, p, h] = jnp.transpose(y[:, h * HEAD:(h + 1) * HEAD]).astype(jnp.bfloat16)
-        w_copy(wq, (SLOTS - k_tiles + p) * TILE, k_tiles + p).start()
         src = vb.at[0, 0, p]
 
         @pl.when(sends_right)
@@ -129,13 +131,24 @@
     def q_tile(n, carry):
         slot = lax.rem(kv_tiles + n, SLOTS)
         w_copy(wq, 0, slot).wait()
+        ahead = lax.rem(kv_tiles + AHEAD + n, SLOTS)
+
+        @pl.when(n + AHEAD < q_tiles)
+        def _():
+            w_copy(wq, (n + AHEAD) * TILE, ahead).start()
+
+        @pl.when(n + AHEAD >= q_tiles)
+        def _():
+            w_copy(wo, (n + AHEAD - q_tiles) * TILE, ahead).start()
+
         y = jnp.dot(xb[...], wbuf[slot], preferred_element_type=jnp.float32).astype(jnp.bfloat16)
         for h in range(PER_TILE):
             q_s[n, h] = y[:, h * HEAD:(h + 1) * HEAD]
-        w_copy(wo, n * TILE, slot).start()
         return carry
 
     lax.fori_loop(0, q_tiles, q_tile, 0)
+    for n in range(AHEAD, o_tiles):
+        w_copy(wo, n * TILE, (kv_tiles + q_tiles + n) % SLOTS).start()
 
     def k_partner(r, p):
         remote(kb.at[r, 0, p], kb.at[r, 1, p], k_send.at[5 + r], kr_p.at[r], partner).start()
@@ -168,7 +181,8 @@
     meta_s[0:n_exp, :] = jnp.where(hits, earlier, -1.0)
     meta_s[n_exp:2 * n_exp, :] = jnp.where(hit0, p0 / total, jnp.where(hit1, p1 / total, 0.0))
 
-    def attend(r, parts, first=False, diagonal=False):
+    def attend(r, parts, lo=0, hi=None, first=False, diagonal=False):
+        hi = q_tiles if hi is None else hi
         keys = parts * tok
         every = pl.ds(0, keys)
         if diagonal:
@@ -213,9 +227,9 @@
         last_h = PER_TILE - 1
 
         def head_group(g, carry):
-            below = jnp.maximum(g - 1, 0)
-            into = lax.select(g == 0, q_tiles, g - 1)
-            above = jnp.minimum(g + 1, q_tiles - 1)
+            below = jnp.maximum(g - 1, lo)
+            into = lax.select(g == lo, q_tiles, g - 1)
+            above = jnp.minimum(g + 1, hi - 1)
             for h in range(PER_TILE):
                 if h < last_h:
                     score(g, h + 1)
@@ -228,9 +242,9 @@
                     apply(below, last_h, into)
             return carry
 
-        score(0, 0)
-        lax.fori_loop(0, q_tiles, head_group, 0)
-        apply(q_tiles - 1, last_h, q_tiles - 1)
+        score(lo, 0)
+        lax.fori_loop(lo, hi, head_group, 0)
+        apply(hi - 1, last_h, hi - 1)
 
     acc[q_tiles, PER_TILE - 1] = jnp.zeros((HEAD, tok), jnp.float32)
     e_b[(PER_TILE - 1) % 2] = jnp.zeros((2 * tok, tok), jnp.bfloat16)
@@ -274,19 +288,27 @@
         got(vb.at[3, 1], kr_p.at[7])
         attend(3, 2)
 
-    @pl.when(gets_right_k)
-    def _():
-        got(kb.at[1, 1], kr_p.at[1])
-        got(vb.at[1, 1], kr_p.at[5])
-        attend(1, 2)
-
-    @pl.when(gets_opp)
-    def _():
+    def take_opp():
         for p in range(k_tiles):
             got(kb.at[2, 0, p], kr_o.at[p])
             k_partner(2, p)
             got(vb.at[2, 0, p], kr_o.at[k_tiles + p])
             v_partner(2, p)
+
+    @pl.when(gets_right_k)
+    def _():
+        got(kb.at[1, 1], kr_p.at[1])
+        got(vb.at[1, 1], kr_p.at[5])
+        attend(1, 2, hi=q_tiles // 2)
+        take_opp()
+        attend(1, 2, lo=q_tiles // 2)
+
+    @pl.when(gets_opp)
+    def _():
+        @pl.when(jnp.logical_not(gets_right_k))
+        def _():
+            take_opp()
+
         got(kb.at[2, 1], kr_p.at[2])
         got(vb.at[2, 1], kr_p.at[6])
         attend(2, 2)
@@ -309,7 +331,7 @@
         return h_all.at[rows_of(dev), pl.ds(col, TILE)]
 
     def o_tile(n, carry):
-        slot = lax.rem(kv_tiles + n, SLOTS)
+        slot = lax.rem(kv_tiles + q_tiles + n, SLOTS)
         w_copy(wo, 0, slot).wait()
         y = jnp.dot(o_s[...], wbuf[slot], preferred_element_type=jnp.float32)
         x = xb[:, pl.ds(pl.multiple_of(n * TILE, TILE), TILE)].astype(jnp.float32)
@@ -322,18 +344,33 @@
 
     lax.fori_loop(0, o_tiles, o_tile, 0)
 
+    def of_chips(which):
+        hit = jnp.bool_(False)
+        for c in which:
+            hit = hit | (chip == c)
+        return hit
+
+    on_right = [[n in VIA_NEXT[(c - 1) % chips] for n in range(o_tiles)] for c in range(chips)]
+    on_left = [[n not in VIA_NEXT[(c + 1) % chips] for n in range(o_tiles)] for c in range(chips)]
+
     def from_left():
         for n in range(o_tiles):
             got(piece(left, n), hr_l.at[n])
-            if n % 2 == 0:
+
+            @pl.when(of_chips([c for c in range(chips) if on_right[c][n]]))
+            def _():
                 remote(piece(left, n), piece(left, n), h_send.at[6], hr_o.at[n], right).start()
+
             remote(piece(left, n), piece(left, n), h_send.at[5], hr_p.at[3], partner).start()
 
     def from_right():
         for n in range(o_tiles):
             got(piece(right, n), hr_r.at[n])
-            if n % 2 == 1:
+
+            @pl.when(of_chips([c for c in range(chips) if on_left[c][n]]))
+            def _():
                 remote(piece(right, n), piece(right, n), h_send.at[7], hr_o.at[n], left).start()
+
             remote(piece(right, n), piece(right, n), h_send.at[3], hr_p.at[1], partner).start()
 
     early_right = (chip == 0) | (chip == last)
@@ -356,8 +393,12 @@
     got(mine, x_sem)
     for i in range(6):
         got(mine, h_send.at[i])
-    for i in (6, 7):
-        got(h_all.at[rows_of(me), pl.ds(0, o_tiles // 2 * TILE)], h_send.at[i])
+    for c in range(chips):
+        @pl.when(chip == c)
+        def _():
+            for i, on in ((6, on_right[c]), (7, on_left[c])):
+                if sum(on):
+                    got(h_all.at[rows_of(me), pl.ds(0, sum(on) * TILE)], h_send.at[i])
     for r in range(chips):
         got(h_all.at[rows_of(lax.rem(partner + 2 * r, group))], hr_p.at[r])
     k_own = kb.at[0, 0]

time: 159 us -> 145 us (0.912)
  Pallas kernels: 158 us -> 144 us
    pallas_call x1, Pallas kernels: 141 us -> 127 us  [device_step(): pl.pallas_call(functools.partial(block_kernel, group, n_exp), out_shape=(...]
where the time goes in v4:
time: 145 us
  Pallas kernels  144 us (99%)
    pallas_call x1, Pallas kernels, device_step(): pl.pallas_call(functools.partial(block_kernel, group, n_exp), out_shape=(...  127 us
    pallas_call x1, Pallas kernels, device_step(): pl.pallas_call(functools.partial(dispatch_kernel, n_exp, own_exp), out_sh...  17.4 us

profile of v4, /device:TPU:81, one launch (start us, length us, event | category | flops | bytes accessed | tf_op | source)
XLA Modules:
  0.0 145.1 jit_solution(1163629783477001794)
XLA Ops:
  0.6 127.1 %block.1 = (bf16[2048,4096]{1,0:T(8,128)(2,1)}, f32[8,32,256]{2,1,0:T(8,128)}) custom-call(bf16[256,4096]{1,0:T(8,128)(2,1)} %x_hbm.1, bf16[4096,4096]{1,0:T(8,128)(2,1)} %wq.1, bf16[4096,1024]{1,0:T(8,128)(2,1)} %wk.1, bf16[4096,1024]{1,0:T(8,128)(2,1)} %wv.1, bf16[4096,4096]{1,0:T(8,128)(2,1)} %wo.1, s32[2,256]{1,0:T(2,128)} %bitcast.3, f32[16,256]{1,0:T(8,128)} %bitcast.2), custom_call_target="tpu_custom_call" | custom-call | tf_op jit(solution)/shard_map/block/pallas_call | solution.py:493
  127.8 17.4 %dispatch.1 = (bf16[256,4096]{1,0:T(8,128)(2,1)}, bf16[2,2048,4096]{2,1,0:T(8,128)(2,1)}) custom-call(f32[8,32,256]{2,1,0:T(8,128)} %get-tuple-element.4.meta_ref, bf16[2048,4096]{1,0:T(8,128)(2,1)} %get-tuple-element.5.h_hbm), custom_call_target="tpu_custom_call" | custom-call | tf_op jit(solution)/shard_map/dispatch/pallas_call | solution.py:524
